TPU v7x, 32 devices: a whole 2x2x4 slice. The times are simulated.
32 devices in a mesh: dp: 2 (over core), vocab: 16 (over z, y, x).
Axes of the slice: x: 2, y: 2, z: 4, core: 2. Of those that a mesh axis runs over, the one named last changes fastest.
Arguments:
- table: bfloat16 [16384, 4096], P('vocab'), may hold values from -0.75 to 0.75
- hidden: bfloat16 [512, 4096], P(('dp', 'vocab')), may hold values from -9 to 9
- cotangent: bfloat16 [512, 4096], P(('dp', 'vocab')), may hold values from -0.75 to 0.75
- input_ids: int32 [512], P('dp'), may hold values from 0 to 16383, as said below
- target_ids: int32 [512], P('dp'), may hold values from 0 to 16383
Outputs:
- table_grad: float32 [16384, 4096], P(('vocab', 'dp'))
- hidden_grad: bfloat16 [512, 4096], P(('dp', 'vocab'))
- token_loss: float32 [512], P('dp')
Inputs may be any that keep to these rules, and one draw needn't show every extreme that they name: `input_ids`: the ids of one replica group may all lie in the 1024 rows of one index of vocab; in every draw some group's ids do.
All inputs are finite; a program needn't handle non-finite values.
Results may differ from a plain program's by a relative error of at most 0.0034.
Values may be sent and summed in bfloat16 or wider, within the bound.
A program may use at most 128 MiB of HBM per device.

v0:
```python
import jax
import jax.numpy as jnp
from jax import lax
from jax.sharding import PartitionSpec as P


def shards(table, hidden, cotangent, input_ids, target_ids):
    shard_rows = table.shape[0]
    width = table.shape[1]
    offset = lax.axis_index("vocab") * shard_rows
    rows = lax.all_gather(hidden, "vocab", axis=0, tiled=True)
    incoming = lax.all_gather(cotangent, "vocab", axis=0, tiled=True)
    logits = lax.dot_general(
        rows, table, (((1,), (1,)), ((), ())), preferred_element_type=jnp.float32
    )
    columns = offset + jnp.arange(shard_rows, dtype=jnp.int32)
    hit = target_ids[:, None] == columns[None, :]
    local_pick = jnp.sum(jnp.where(hit, logits, jnp.float32(0.0)), axis=1)
    local_max = jnp.max(logits, axis=1)
    top = lax.pmax(local_max, "vocab")
    local_total = jnp.sum(jnp.exp(logits - top[:, None]), axis=1)
    total, picked = lax.psum((local_total, local_pick), "vocab")
    lse = top + jnp.log(total)
    token_loss = lse - picked
    dlogits = (jnp.exp(logits - lse[:, None]) - hit.astype(jnp.float32)).astype(jnp.bfloat16)
    hidden_grad = lax.psum_scatter(
        jnp.dot(dlogits, table, preferred_element_type=jnp.float32),
        "vocab",
        scatter_dimension=0,
        tiled=True,
    ).astype(jnp.bfloat16)
    local_ids = input_ids - offset
    inside = (local_ids >= 0) & (local_ids < shard_rows)
    targets = jnp.where(inside, local_ids, shard_rows)
    first_section = (
        jnp.zeros((shard_rows, width), jnp.float32)
        .at[targets]
        .add(incoming.astype(jnp.float32), mode="drop")
    )
    full = (
        lax.dot_general(dlogits, rows, (((0,), (0,)), ((), ())), preferred_element_type=jnp.float32)
        + first_section
    )
    table_grad = lax.psum_scatter(full, "dp", scatter_dimension=0, tiled=True)
    return (table_grad, hidden_grad, token_loss)


def solution(mesh):
    return jax.shard_map(
        shards,
        mesh=mesh,
        in_specs=(
            P("vocab", None),
            P(("dp", "vocab"), None),
            P(("dp", "vocab"), None),
            P("dp"),
            P("dp"),
        ),
        out_specs=(P(("vocab", "dp"), None), P(("dp", "vocab"), None), P("dp")),
        check_vma=False,
    )
```

profile of v0, /device:TPU:0, one launch (start us, length us, event | category | flops | bytes accessed | tf_op | source)
XLA Modules:
  0.0 292.8 jit_solution(14492816868424003785)
XLA Ops:
  7.2 0.0 all-gather.3.cloned.1.call-start
  7.2 0.7 all-gather.3.cloned.1.call-update
  7.9 0.0 all-gather.5.cloned.1.call-start
  7.9 0.7 all-gather.5.cloned.1.call-update
  8.6 0.0 reduce-scatter.5.cloned.1.call-start
  8.7 0.0 copy-start.1
  8.7 65.2 %all-gather.3.cloned.1.call-done = bf16[256,4096]{1,0:T(8,128)(2,1)} async-done(((bf16[16,4096]{1,0:T(8,128)(2,1)}), bf16[256,4096]{1,0:T(8,128)(2,1)}) %all-gather.3.cloned.1.call-update) | async-done | bytes 2097168 | tf_op jit(solution)/shard_map/all_gather | solution.py:11
  73.9 6.5 %fusion.10 = (f32[256]{0:T(256)S(1)}, f32[256,1024]{1,0:T(8,128)S(1)}) fusion(bf16[256,4096]{1,0:T(8,128)(2,1)} %all-gather.3.cloned.1.call-done, bf16[1024,4096]{1,0:T(8,128)(2,1)} %param.5), kind=kOutput, calls=%fused_computation.16 | convolution fusion | flops 2147745536 | bytes 11535360 | tf_op jit(solution)/shard_map/dot_general | solution.py:13
  80.3 39.8 %pmax.7 = f32[256]{0:T(256)S(1)} all-reduce(f32[256]{0:T(256)S(1)} %get-tuple-element.9), channel_id=1, replica_groups=mesh['dp'=2,'vocab'=16] {'vocab'}, use_global_device_ids=true, to_apply=%region_1.2 | all-reduce | flops 256 | bytes 2048 | tf_op jit(solution)/shard_map/pmax | solution.py:20
  120.2 0.0 copy-done.1
  120.2 0.4 fusion.4
  120.6 36.9 %all-reduce = (f32[256]{0:T(256)S(1)}, f32[256]{0:T(256)S(1)}) all-reduce(f32[256]{0:T(256)S(1)} %get-tuple-element.4, f32[256]{0:T(256)S(1)} %get-tuple-element.3), channel_id=1, replica_groups=mesh['dp'=2,'vocab'=16] {'vocab'}, use_global_device_ids=true, to_apply=%region_3.4 | all-reduce | flops 512 | bytes 4096 | tf_op jit(solution)/shard_map/psum | solution.py:22
  157.4 0.6 fusion.9
  158.0 7.8 %fusion.5 = f32[256,4096]{1,0:T(8,128)} fusion(bf16[1024,4096]{1,0:T(8,128)(2,1)} %param.5, f32[256,1024]{1,0:T(8,128)S(1)} %get-tuple-element.10, s32[1024]{0:T(1024)S(1)} %iota_add_fusion, f32[256]{0:T(256)S(1)} %get-tuple-element.8, s32[256]{0:T(256)S(1)} %copy-done.1), kind=kOutput, calls=%fused_computation.13 | convolution fusion | flops 2148794368 | bytes 13637632 | tf_op jit(solution)/shard_map/dot_general | solution.py:27
  165.8 0.0 copy-start.2
  165.8 0.0 copy-start
  165.8 0.0 reduce-scatter.5.cloned.1.call-update
  165.8 0.2 reduce-scatter.3.cloned.1.call-start
  166.1 0.4 copy-done.2
  166.5 0.9 copy-done
  167.4 8.2 %fusion.7 = f32[1024,4096]{1,0:T(8,128)} fusion(bf16[256,4096]{1,0:T(8,128)(2,1)S(1)} %copy-done, f32[256,1024]{1,0:T(8,128)S(1)} %get-tuple-element.10, s32[1024]{0:T(1024)S(1)} %iota_add_fusion, f32[256]{0:T(256)S(1)} %get-tuple-element.8, s32[256]{0:T(256)S(1)} %copy-done.1), kind=kOutput, calls=%fused_computation.14 | convolution fusion | flops 2148794368 | bytes 19929088 | tf_op jit(solution)/shard_map/dot_general | solution.py:41
  175.6 0.0 all-gather.5.cloned.1.call-done
  175.6 18.7 %scatter_custom_fusion = f32[1024,4096]{1,0:T(8,128)} fusion(f32[1024,4096]{1,0:T(8,128)} %fusion.7, s32[256]{0:T(256)S(1)} %compare_select_fusion.1, bf16[256,4096]{1,0:T(8,128)(2,1)} %all-gather.5.cloned.1.call-done), kind=kCustom, calls=%fused_computation.1 | custom fusion | flops 2097152 | bytes 18874368 | tf_op jit(solution)/shard_map/scatter-add | solution.py:38
  194.4 0.0 reduce-scatter.3.cloned.1.call-update
  194.4 64.5 %reduce-scatter.5.cloned.1.call-done = f32[16,4096]{1,0:T(8,128)} async-done(((f32[256,4096]{1,0:T(8,128)}), f32[16,4096]{1,0:T(8,128)}) %reduce-scatter.5.cloned.1.call-update) | async-done | bytes 262160 | tf_op jit(solution)/shard_map/reduce_scatter | solution.py:26
  258.9 1.6 convert_element_type.15
  260.5 25.7 %reduce-scatter.3.cloned.1.call-done = f32[512,4096]{1,0:T(8,128)} async-done(((f32[1024,4096]{1,0:T(8,128)}), f32[512,4096]{1,0:T(8,128)}) %reduce-scatter.3.cloned.1.call-update) | async-done | bytes 8388624 | tf_op jit(solution)/shard_map/reduce_scatter | solution.py:44
  (2 shorter events, 0.0 us)
Async XLA Ops:
  7.2 66.7 %all-gather.3.cloned.1.call-start = ((), (), s32[]{:S(2)}) async-start(), calls=%async_computation.2 | async-start | bytes 2228224 | tf_op jit(solution)/shard_map/all_gather | solution.py:11
  7.9 167.7 %all-gather.5.cloned.1.call-start = ((), (), s32[]{:S(2)}) async-start(), calls=%async_computation.3 | async-start | bytes 2228224 | tf_op jit(solution)/shard_map/all_gather | solution.py:12
  8.6 250.2 %reduce-scatter.5.cloned.1.call-start = ((), (), s32[]{:S(2)}) async-start(), calls=%async_computation.5 | async-start | bytes 4456448 | tf_op jit(solution)/shard_map/reduce_scatter | solution.py:26
  8.7 111.4 %copy-start.1 = (s32[256]{0:T(256)S(1)}, s32[256]{0:T(256)}, u32[]{:S(2)}) copy-start(s32[256]{0:T(256)} %param.9) | copy-start | bytes 3076
  165.8 0.7 copy-start.2
  165.8 1.6 copy-start
  165.8 120.4 %reduce-scatter.3.cloned.1.call-start = ((), (), s32[]{:S(2)}) async-start(), calls=%async_computation.4 | async-start | bytes 25165824 | tf_op jit(solution)/shard_map/reduce_scatter | solution.py:44
Sparse Core Ops, SparseCore 0:
  10.7 63.0 all-gather.2
  76.6 59.4 all-gather.4
  165.9 92.8 reduce-scatter.4
  261.6 24.5 reduce-scatter.2
where the time goes:
time: 293 us
  waiting for transfers between devices  157 us (54%)
  blocking collectives  76.7 us (26%)
  matrix products  22.5 us (8%)
  other arithmetic  21.3 us (7%)
  between operations  13.8 us (5%)
    all_gather x1, waiting for transfers between devices, shards(): rows = lax.all_gather(hidden, 'vocab', axis=0, tiled=True)  65.2 us
    reduce_scatter x1, waiting for transfers between devices, shards(): lax.psum_scatter(jnp.dot(dlogits, table, preferred_element_type=jnp.float...  64.5 us
    pmax x1, blocking collectives, shards(): top = lax.pmax(local_max, 'vocab')  39.8 us
    psum x1, blocking collectives, shards(): total, picked = lax.psum((local_total, local_pick), 'vocab')  36.9 us
    reduce_scatter x1, waiting for transfers between devices, shards(): table_grad = lax.psum_scatter(full, 'dp', scatter_dimension=0, tiled=True)  25.7 us
    scatter-add x1, other arithmetic, shards(): first_section = jnp.zeros((shard_rows, width), jnp.float32).at[targets].a...  18.7 us
    dot_general x1, matrix products, shards(): lax.dot_general(dlogits, rows, (((0,), (0,)), ((), ())), preferred_elemen...  8.23 us
    dot_general x1, matrix products, shards(): jnp.dot(dlogits, table, preferred_element_type=jnp.float32)  7.77 us
  transfers between devices with their start and end apart: 4, of which 3 were waited for; matrix products, arithmetic and copies ran while one was open for 15% of the time, Pallas kernels for 0%

commit v1 on v0

--- a/solution.py
+++ b/solution.py
@@ -8,8 +8,11 @@
     shard_rows = table.shape[0]
     width = table.shape[1]
     offset = lax.axis_index("vocab") * shard_rows
-    rows = lax.all_gather(hidden, "vocab", axis=0, tiled=True)
-    incoming = lax.all_gather(cotangent, "vocab", axis=0, tiled=True)
+    rows, incoming = jnp.split(
+        lax.all_gather(jnp.concatenate([hidden, cotangent], axis=1), "vocab", axis=0, tiled=True),
+        [hidden.shape[1]],
+        axis=1,
+    )
     logits = lax.dot_general(
         rows, table, (((1,), (1,)), ((), ())), preferred_element_type=jnp.float32
     )

time: 293 us -> 308 us (1.051)
  waiting for transfers between devices: 157 us -> 171 us
    all_gather x2 -> x1, waiting for transfers between devices: 65.2 us -> 80.7 us  [shards(): lax.all_gather(jnp.concatenate([hidden, cotangent], axis=1), 'vocab', axi...]
  transfers between devices with their start and end apart: 4 -> 3, of which waited for: 3 -> 3; matrix products, arithmetic and copies ran while one was open for 15% -> 10% of each run, Pallas kernels for 0% -> 0%
where the time goes in v1:
time: 308 us
  waiting for transfers between devices  171 us (56%)
  blocking collectives  75.9 us (25%)
  matrix products  24.1 us (8%)
  other arithmetic  23 us (7%)
  between operations  13.8 us (4%)
    all_gather x1, waiting for transfers between devices, shards(): lax.all_gather(jnp.concatenate([hidden, cotangent], axis=1), 'vocab', axi...  80.7 us
    reduce_scatter x1, waiting for transfers between devices, shards(): lax.psum_scatter(jnp.dot(dlogits, table, preferred_element_type=jnp.float...  64 us
    pmax x1, blocking collectives, shards(): top = lax.pmax(local_max, 'vocab')  39.4 us
    psum x1, blocking collectives, shards(): total, picked = lax.psum((local_total, local_pick), 'vocab')  36.6 us
    reduce_scatter x1, waiting for transfers between devices, shards(): table_grad = lax.psum_scatter(full, 'dp', scatter_dimension=0, tiled=True)  25.9 us
    scatter-add x1, other arithmetic, shards(): first_section = jnp.zeros((shard_rows, width), jnp.float32).at[targets].a...  18.7 us
    dot_general x1, matrix products, shards(): lax.dot_general(dlogits, rows, (((0,), (0,)), ((), ())), preferred_elemen...  9.82 us
    dot_general x1, matrix products, shards(): jnp.dot(dlogits, table, preferred_element_type=jnp.float32)  7.78 us
  transfers between devices with their start and end apart: 3, of which 3 were waited for; matrix products, arithmetic and copies ran while one was open for 10% of the time, Pallas kernels for 0%

profile of v1, /device:TPU:0, one launch (start us, length us, event | category | flops | bytes accessed | tf_op | source)
XLA Modules:
  0.0 308.1 jit_solution(10558892179661774579)
XLA Ops:
  7.2 0.0 all-gather.2.cloned.1.call-start
  7.2 1.7 pad_maximum_fusion
  8.9 0.0 all-gather.2.cloned.1.call-update
  8.9 0.0 reduce-scatter.5.cloned.1.call-start
  9.0 0.0 copy-start
  9.0 80.7 %all-gather.2.cloned.1.call-done = bf16[256,8192]{1,0:T(8,128)(2,1)} async-done(((bf16[16,8192]{1,0:T(8,128)(2,1)}), bf16[256,8192]{1,0:T(8,128)(2,1)}) %all-gather.2.cloned.1.call-update) | async-done | bytes 4194320 | tf_op jit(solution)/shard_map/all_gather | solution.py:12
  89.7 6.5 %fusion.14 = (f32[256]{0:T(256)S(1)}, f32[256,1024]{1,0:T(8,128)S(1)}) fusion(bf16[1024,4096]{1,0:T(8,128)(2,1)} %param.5, bf16[256,8192]{1,0:T(8,128)(2,1)} %all-gather.2.cloned.1.call-done), kind=kOutput, calls=%fused_computation.21 | convolution fusion | flops 2147745536 | bytes 11535360 | tf_op jit(solution)/shard_map/dot_general | solution.py:16
  96.1 39.4 %pmax.7 = f32[256]{0:T(256)S(1)} all-reduce(f32[256]{0:T(256)S(1)} %get-tuple-element.9), channel_id=1, replica_groups=mesh['dp'=2,'vocab'=16] {'vocab'}, use_global_device_ids=true, to_apply=%region_1.2 | all-reduce | flops 256 | bytes 2048 | tf_op jit(solution)/shard_map/pmax | solution.py:23
  135.5 0.0 copy-done
  135.5 0.4 fusion.9
  135.9 36.6 %all-reduce = (f32[256]{0:T(256)S(1)}, f32[256]{0:T(256)S(1)}) all-reduce(f32[256]{0:T(256)S(1)} %get-tuple-element.4, f32[256]{0:T(256)S(1)} %get-tuple-element.3), channel_id=1, replica_groups=mesh['dp'=2,'vocab'=16] {'vocab'}, use_global_device_ids=true, to_apply=%region_3.4 | all-reduce | flops 512 | bytes 4096 | tf_op jit(solution)/shard_map/psum | solution.py:25
  172.5 0.6 fusion.13
  173.0 7.8 %fusion.10 = f32[256,4096]{1,0:T(8,128)} fusion(bf16[1024,4096]{1,0:T(8,128)(2,1)} %param.5, f32[256,1024]{1,0:T(8,128)S(1)} %get-tuple-element.10, s32[1024]{0:T(1024)S(1)} %iota_add_fusion, f32[256]{0:T(256)S(1)} %get-tuple-element.8, s32[256]{0:T(256)S(1)} %copy-done), kind=kOutput, calls=%fused_computation.19 | convolution fusion | flops 2148794368 | bytes 13637632 | tf_op jit(solution)/shard_map/dot_general | solution.py:30
  180.8 0.0 copy-start.1
  180.8 0.0 reduce-scatter.5.cloned.1.call-update
  180.9 0.2 reduce-scatter.3.cloned.1.call-start
  181.1 0.4 copy-done.1
  181.5 9.8 %fusion.3 = f32[1024,4096]{1,0:T(8,128)} fusion(bf16[256,8192]{1,0:T(8,128)(2,1)} %all-gather.2.cloned.1.call-done, f32[256,1024]{1,0:T(8,128)S(1)} %get-tuple-element.10, s32[1024]{0:T(1024)S(1)} %iota_add_fusion, f32[256]{0:T(256)S(1)} %get-tuple-element.8, s32[256]{0:T(256)S(1)} %copy-done), kind=kOutput, calls=%fused_computation.4 | convolution fusion | flops 2148794368 | bytes 19929088 | tf_op jit(solution)/shard_map/dot_general | solution.py:44
  191.3 18.7 %scatter_custom_fusion = f32[1024,4096]{1,0:T(8,128)} fusion(f32[1024,4096]{1,0:T(8,128)} %fusion.3, s32[256]{0:T(256)S(1)} %compare_select_fusion.1, bf16[256,8192]{1,0:T(8,128)(2,1)} %all-gather.2.cloned.1.call-done), kind=kCustom, calls=%fused_computation.1 | custom fusion | flops 2097152 | bytes 18874368 | tf_op jit(solution)/shard_map/scatter-add | solution.py:41
  210.1 0.0 reduce-scatter.3.cloned.1.call-update
  210.1 64.0 %reduce-scatter.5.cloned.1.call-done = f32[16,4096]{1,0:T(8,128)} async-done(((f32[256,4096]{1,0:T(8,128)}), f32[16,4096]{1,0:T(8,128)}) %reduce-scatter.5.cloned.1.call-update) | async-done | bytes 262160 | tf_op jit(solution)/shard_map/reduce_scatter | solution.py:29
  274.1 1.6 convert_element_type.15
  275.7 25.9 %reduce-scatter.3.cloned.1.call-done = f32[512,4096]{1,0:T(8,128)} async-done(((f32[1024,4096]{1,0:T(8,128)}), f32[512,4096]{1,0:T(8,128)}) %reduce-scatter.3.cloned.1.call-update) | async-done | bytes 8388624 | tf_op jit(solution)/shard_map/reduce_scatter | solution.py:47
  (2 shorter events, 0.0 us)
Async XLA Ops:
  7.2 82.5 %all-gather.2.cloned.1.call-start = ((), (), s32[]{:S(2)}) async-start(), calls=%async_computation.2 | async-start | bytes 4456448 | tf_op jit(solution)/shard_map/all_gather | solution.py:12
  8.9 265.2 %reduce-scatter.5.cloned.1.call-start = ((), (), s32[]{:S(2)}) async-start(), calls=%async_computation.4 | async-start | bytes 4456448 | tf_op jit(solution)/shard_map/reduce_scatter | solution.py:29
  9.0 126.5 %copy-start = (s32[256]{0:T(256)S(1)}, s32[256]{0:T(256)}, u32[]{:S(2)}) copy-start(s32[256]{0:T(256)} %param.9) | copy-start | bytes 3076
  180.8 0.7 copy-start.1
  180.9 120.7 %reduce-scatter.3.cloned.1.call-start = ((), (), s32[]{:S(2)}) async-start(), calls=%async_computation.3 | async-start | bytes 25165824 | tf_op jit(solution)/shard_map/reduce_scatter | solution.py:47
Sparse Core Ops, SparseCore 0:
  11.3 78.3 all-gather.1
  181.0 93.0 reduce-scatter.4
  277.0 24.5 reduce-scatter.2
